TPU v7x, 32 devices: a whole 2x2x4 slice. The times are simulated.
32 devices in a mesh: row: 8 (over z, core), col: 4 (over y, x).
Axes of the slice: x: 2, y: 2, z: 4, core: 2. Of those that a mesh axis runs over, the one named last changes fastest.
Arguments:
- embedding: bfloat16 [256, 128], P('col'), may hold values from -6 to 6
- dilation: int32 [2], replicated, may hold values from 1 to 4, as said below
- kernel: bfloat16 [3, 3, 48, 128], replicated, may hold values from -0.1875 to 0.1875
- kernel_bias: float32 [48], replicated, may hold values from -3 to 3
- mixing: bfloat16 [5, 48], replicated, may hold values from -0.875 to 0.875
- mixing_bias: float32 [5], replicated, may hold values from -3 to 3
- cotangent: bfloat16 [5, 256, 256], P(None, 'row', 'col'), may hold values from -0.375 to 0.375
Outputs:
- contact: float32 [5, 256, 256], P(None, 'row', 'col')
- embedding_grad: float32 [256, 128], P('col')
- kernel_grad: float32 [3, 3, 48, 128], replicated
Inputs may be any that keep to these rules, and one draw needn't show every extreme that they name: `dilation`: the larger of the two rates is exactly 4.
All inputs are finite; a program needn't handle non-finite values.
Results may differ from a plain program's by a relative error of at most 0.019.
The roundings to bfloat16 on the way count: a program that leaves them out, or rounds other values in their place, can miss the bound.
Values may be sent and summed in bfloat16 or wider, within the bound.
No kernel may reach another device: no remote copies, remote signals or barrier semaphores. Data moves between devices by JAX's collectives and lax.ppermute only.
A program may use at most 64 MiB of HBM per device.

v0:
```python
import jax
import jax.numpy as jnp
from jax import lax
from jax.sharding import PartitionSpec as P

DMAX = 4


def shifted(value, axis, by):
    peers = lax.axis_size(axis)
    pairs = [(i, i + by) for i in range(peers) if 0 <= i + by < peers]
    return lax.ppermute(value, axis, pairs)


def tap_list():
    return [(tap_row, tap_col) for tap_row in (-1, 0, 1) for tap_col in (-1, 0, 1)]


def narrow(values):
    return values.astype(jnp.bfloat16)


def add_into(target, position, update):
    current = lax.dynamic_slice_in_dim(target, position, update.shape[0], 0)
    return lax.dynamic_update_slice_in_dim(target, current + update, position, 0)


def fold_edges(extended, margin, count, before, after):
    inner_rows = extended[margin : margin + count]
    inner_rows = inner_rows + jnp.pad(before, ((0, count - margin), (0, 0)))
    return inner_rows + jnp.pad(after, ((count - margin, 0), (0, 0)))


def per_device(embedding, dilation, kernel, kernel_bias, mixing, mixing_bias, cotangent):
    highest = lax.Precision.HIGHEST
    row_rate = dilation[0]
    col_rate = dilation[1]
    margin = DMAX
    channels = embedding.shape[1]
    filters = kernel.shape[2]
    row_count = cotangent.shape[1]
    col_count = cotangent.shape[2]
    col_devices = lax.axis_size("col")
    bins_total = col_count * col_devices
    row_index = lax.axis_index("row")
    col_index = lax.axis_index("col")
    row_start = row_index * row_count
    col_start = col_index * col_count
    every_bin = lax.all_gather(embedding, "col", axis=0, tiled=True)
    padded = jnp.pad(every_bin, ((margin, margin), (0, 0)))
    row_values = lax.dynamic_slice_in_dim(padded, row_start, row_count + 2 * margin, 0)
    col_values = lax.dynamic_slice_in_dim(padded, col_start, col_count + 2 * margin, 0)
    row_places = row_start - margin + jnp.arange(row_count + 2 * margin, dtype=jnp.int32)
    col_places = col_start - margin + jnp.arange(col_count + 2 * margin, dtype=jnp.int32)
    row_inside = ((row_places >= 0) & (row_places < bins_total)).astype(jnp.float32)
    col_inside = ((col_places >= 0) & (col_places < bins_total)).astype(jnp.float32)
    pairs = narrow(
        0.5
        * (row_values.astype(jnp.float32)[:, None, :] + col_values.astype(jnp.float32)[None, :, :])
    )
    keep_mask = (row_inside[:, None] * col_inside[None, :]).astype(jnp.bfloat16)
    pairs = pairs * keep_mask[:, :, None]
    zero_index = jnp.zeros((), jnp.int32)

    def slicer(tap_row, tap_col, mirrored):
        if mirrored:
            first_at, second_at = (margin + tap_col * col_rate, margin + tap_row * row_rate)
        else:
            first_at, second_at = (margin + tap_row * row_rate, margin + tap_col * col_rate)
        return lax.dynamic_slice(
            pairs, (first_at, second_at, zero_index), (row_count, col_count, channels)
        )

    def convolve(mirrored):
        running = jnp.zeros((filters, row_count, col_count), jnp.float32)
        for tap_row, tap_col in tap_list():
            tap_piece = slicer(tap_row, tap_col, mirrored)
            running = running + jnp.einsum(
                "ijc,fc->fij",
                tap_piece,
                kernel[tap_row + 1, tap_col + 1],
                preferred_element_type=jnp.float32,
            )
        return running + kernel_bias[:, None, None]

    direct = convolve(False)
    mirror = convolve(True)
    direct_act = narrow(jax.nn.relu(direct))
    mirror_act = narrow(jax.nn.relu(mirror))

    def mix_map(activation):
        return (
            jnp.einsum("tf,fij->tij", mixing, activation, preferred_element_type=jnp.float32)
            + mixing_bias[:, None, None]
        )

    contact = 0.5 * mix_map(direct_act) + 0.5 * mix_map(mirror_act)
    guide_grad = narrow(
        0.5 * jnp.einsum("tf,tij->fij", mixing, cotangent, preferred_element_type=jnp.float32)
    )
    grad_direct = jnp.where(direct > 0, guide_grad, jnp.zeros_like(guide_grad))
    grad_mirror = jnp.where(mirror > 0, guide_grad, jnp.zeros_like(guide_grad))
    updates = []
    for tap_row, tap_col in tap_list():
        tap_term = jnp.einsum(
            "fij,ijc->fc",
            grad_direct,
            slicer(tap_row, tap_col, False),
            preferred_element_type=jnp.float32,
        )
        tap_term = tap_term + jnp.einsum(
            "fij,ijc->fc",
            grad_mirror,
            slicer(tap_row, tap_col, True),
            preferred_element_type=jnp.float32,
        )
        updates.append(tap_term)
    kernel_terms = jnp.stack(updates).reshape(3, 3, filters, channels)
    kernel_grad = lax.psum(kernel_terms, ("row", "col"))

    def col_mask(shift):
        return lax.dynamic_slice_in_dim(col_inside, margin + shift, col_count, 0).astype(
            jnp.bfloat16
        )

    def row_mask(shift):
        return lax.dynamic_slice_in_dim(row_inside, margin + shift, row_count, 0).astype(
            jnp.bfloat16
        )

    direct_rows = [
        jnp.einsum(
            "fij,j->fi",
            grad_direct,
            col_mask(tap_step * col_rate),
            preferred_element_type=jnp.float32,
        )
        for tap_step in (-1, 0, 1)
    ]
    direct_cols = [
        jnp.einsum(
            "fij,i->fj",
            grad_direct,
            row_mask(tap_step * row_rate),
            preferred_element_type=jnp.float32,
        )
        for tap_step in (-1, 0, 1)
    ]
    mirror_rows = [
        jnp.einsum(
            "fij,j->fi",
            grad_mirror,
            col_mask(tap_step * row_rate),
            preferred_element_type=jnp.float32,
        )
        for tap_step in (-1, 0, 1)
    ]
    mirror_cols = [
        jnp.einsum(
            "fij,i->fj",
            grad_mirror,
            row_mask(tap_step * col_rate),
            preferred_element_type=jnp.float32,
        )
        for tap_step in (-1, 0, 1)
    ]
    row_grad = jnp.zeros((row_count + 2 * margin, channels), jnp.float32)
    col_grad = jnp.zeros((col_count + 2 * margin, channels), jnp.float32)
    for tap_row, tap_col in tap_list():
        tap_weight = kernel[tap_row + 1, tap_col + 1].astype(jnp.float32)
        row_grad = add_into(
            row_grad,
            margin + tap_row * row_rate,
            jnp.einsum("fi,fc->ic", direct_rows[tap_col + 1], tap_weight, precision=highest),
        )
        row_grad = add_into(
            row_grad,
            margin + tap_col * col_rate,
            jnp.einsum("fi,fc->ic", mirror_rows[tap_row + 1], tap_weight, precision=highest),
        )
        col_grad = add_into(
            col_grad,
            margin + tap_col * col_rate,
            jnp.einsum("fj,fc->jc", direct_cols[tap_row + 1], tap_weight, precision=highest),
        )
        col_grad = add_into(
            col_grad,
            margin + tap_row * row_rate,
            jnp.einsum("fj,fc->jc", mirror_cols[tap_col + 1], tap_weight, precision=highest),
        )
    upper_rows = shifted(row_grad[:margin], "row", -1)
    lower_rows = shifted(row_grad[row_count + margin :], "row", 1)
    inner_rows = fold_edges(row_grad, margin, row_count, lower_rows, upper_rows)
    row_total = lax.psum(inner_rows, "col")
    every_row = lax.all_gather(row_total, "row", axis=0, tiled=True)
    row_share = lax.dynamic_slice_in_dim(every_row, col_start, col_count, 0)
    left_cols = shifted(col_grad[:margin], "col", -1)
    right_cols = shifted(col_grad[col_count + margin :], "col", 1)
    inner_cols = fold_edges(col_grad, margin, col_count, right_cols, left_cols)
    col_total = lax.psum(inner_cols, "row")
    embedding_grad = 0.5 * row_share + 0.5 * col_total
    return (contact, embedding_grad, kernel_grad)


def solution(mesh):
    return jax.shard_map(
        per_device,
        mesh=mesh,
        in_specs=(P("col", None), P(), P(), P(), P(), P(), P(None, "row", "col")),
        out_specs=(P(None, "row", "col"), P("col", None), P()),
        check_vma=False,
    )
```

profile of v0, /device:TPU:8, one launch (start us, length us, event | category | flops | bytes accessed | tf_op | source)
XLA Modules:
  0.0 207.0 jit_solution(6077568537397466937)
XLA Ops:
  7.2 1.3 fusion.300
  13.8 8.4 %all_gather.6 = bf16[256,128]{1,0:T(8,128)(2,1)S(1)} all-gather(bf16[64,128]{1,0:T(8,128)(2,1)} %param.7), channel_id=1, replica_groups=mesh['row'=8,'col'=4] {'col'}, dimensions={0}, use_global_device_ids=true | all-gather | bytes 81920 | tf_op jit(solution)/shard_map/all_gather | solution.py:49
  22.3 0.5 fusion.35
  22.8 0.6 fusion.72
  23.4 0.6 fusion.68
  24.0 0.6 convolution_add_fusion.13
  24.7 0.6 convolution_add_fusion.12
  25.3 0.6 fusion.3
  26.0 0.6 convolution_add_fusion.10
  26.6 0.6 convolution_add_fusion.9
  27.2 0.6 convolution_add_fusion.8
  27.9 0.6 fusion.59
  28.5 0.6 convolution_add_fusion.6
  29.1 0.6 convolution_add_fusion.5
  29.8 0.5 copy-done.3
  30.3 0.6 fusion.1
  30.9 0.6 convolution_add_fusion.3
  31.5 0.6 convolution_add_fusion.2
  32.2 0.6 convolution_add_fusion.1
  32.8 0.6 fusion.2
  33.4 0.6 fusion
  34.1 0.4 bitcast_select_fusion
  36.0 0.3 dynamic_update_slice.126
  36.5 0.3 dynamic_update_slice.127
  37.4 0.3 dynamic_update_slice.129
  37.9 0.3 dynamic_update_slice.130
  38.4 0.3 dynamic_update_slice.131
  38.9 0.3 dynamic_update_slice.132
  44.9 1.3 collective-permute-start.3
  46.2 4.7 %collective-permute-start.2 = (f32[4,128]{1,0:T(4,128)S(1)}, f32[4,128]{1,0:T(4,128)S(1)}, u32[]{:S(2)}, u32[]{:S(2)}) collective-permute-start(f32[4,128]{1,0:T(4,128)S(1)} %get-tuple-element.8), channel_id=1, source_target_pairs={{0,1},{1,2},{2,3},{4,5},{5,6},{6,7},{8,9},{9,10},{10,11},{12,13},{... | collective-permute-start | bytes 6152 | tf_op jit(solution)/shard_map/ppermute | solution.py:12
  50.9 0.5 fusion.272
  51.4 0.5 fusion.270
  51.9 0.5 fusion.264
  52.4 0.5 fusion.268
  52.9 0.5 fusion.266
  56.5 0.5 fusion.262
  59.9 1.9 collective-permute-start.1
  61.8 2.4 %collective-permute-start = (f32[4,128]{1,0:T(4,128)S(1)}, f32[4,128]{1,0:T(4,128)S(1)}, u32[]{:S(2)}, u32[]{:S(2)}) collective-permute-start(f32[4,128]{1,0:T(4,128)S(1)} %get-tuple-element.10), channel_id=1, source_target_pairs={{0,4},{4,8},{8,12},{12,16},{16,20},{20,24},{24,28},{1,5},{5,9},{9,... | collective-permute-start | bytes 6152 | tf_op jit(solution)/shard_map/ppermute | solution.py:12
  64.2 0.3 convolution_bitcast_fusion.16
  64.5 0.3 convolution_bitcast_fusion.14
  64.8 0.3 convolution_bitcast_fusion.12
  65.2 0.3 convolution_bitcast_fusion.10
  65.5 0.3 convolution_bitcast_fusion.8
  65.8 0.3 convolution_bitcast_fusion.6
  66.1 0.3 convolution_bitcast_fusion.4
  66.5 0.3 convolution_bitcast_fusion.2
  66.8 0.3 convolution_bitcast_fusion
  67.1 0.3 fusion.10
  67.4 0.3 fusion.13
  67.8 0.3 fusion.16
  68.1 0.3 fusion.19
  68.4 0.3 fusion.22
  68.8 0.3 fusion.25
  69.1 0.3 fusion.28
  69.4 0.3 fusion.31
  69.8 0.3 fusion.34
  70.1 0.7 copy-done.4
  71.2 0.7 copy.11
  71.8 24.8 %psum.22 = f32[64,128]{1,0:T(8,128)S(1)} all-reduce(f32[64,128]{1,0:T(8,128)S(1)} %fusion.93), channel_id=1, replica_groups=mesh['row'=8,'col'=4] {'row'}, use_global_device_ids=true, to_apply=%region_1.2 | all-reduce | flops 8192 | bytes 65536 | tf_op jit(solution)/shard_map/psum | solution.py:200
  96.7 15.8 %psum.21 = f32[32,128]{1,0:T(8,128)S(1)} all-reduce(f32[32,128]{1,0:T(8,128)S(1)} %fusion.95), channel_id=1, replica_groups=mesh['row'=8,'col'=4] {'col'}, use_global_device_ids=true, to_apply=%region_0.1 | all-reduce | flops 4096 | bytes 32768 | tf_op jit(solution)/shard_map/psum | solution.py:194
  112.5 14.2 %all_gather.7 = f32[256,128]{1,0:T(8,128)S(1)} all-gather(f32[32,128]{1,0:T(8,128)S(1)} %psum.21), channel_id=1, replica_groups=mesh['row'=8,'col'=4] {'row'}, dimensions={0}, use_global_device_ids=true | all-gather | bytes 147456 | tf_op jit(solution)/shard_map/all_gather | solution.py:195
  126.7 0.6 add_multiply_fusion
  127.3 71.2 %all-reduce.7.cloned.1.call-done = f32[3,3,48,128]{3,2,1,0:T(8,128)} async-done(((f32[3,3,48,128]{3,2,1,0:T(8,128)}), f32[3,3,48,128]{3,2,1,0:T(8,128)}) %all-reduce.7.cloned.1.call-update) | async-done | bytes 221200 | tf_op jit(solution)/shard_map/psum | solution.py:119
  198.5 1.6 copy.87
  (107 shorter events, 14.9 us)
Async XLA Ops:
  7.2 26.9 %copy-start = (bf16[5,32,64]{2,1,0:T(8,128)(2,1)S(1)}, bf16[5,32,64]{2,1,0:T(8,128)(2,1)}, u32[]{:S(2)}) copy-start(bf16[5,32,64]{2,1,0:T(8,128)(2,1)} %param.13) | copy-start | bytes 61444
  7.2 15.6 %copy-start.1 = (bf16[3,3,48,128]{3,2,1,0:T(8,128)(2,1)S(1)}, bf16[3,3,48,128]{3,2,1,0:T(8,128)(2,1)}, u32[]{:S(2)}) copy-start(bf16[3,3,48,128]{3,2,1,0:T(8,128)(2,1)} %param.9) | copy-start | bytes 331780
  7.2 191.3 %all-reduce.7.cloned.1.call-start = ((), (), s32[]{:S(2)}) async-start(), calls=%async_computation | async-start | bytes 442368 | tf_op jit(solution)/shard_map/psum | solution.py:119
  23.4 1.9 copy-start.2
  29.1 1.1 copy-start.3
  32.2 0.7 copy-start.6
  33.4 0.7 copy-start.5
  44.9 27.0 %collective-permute-start.3 = (f32[4,128]{1,0:T(4,128)S(1)}, f32[4,128]{1,0:T(4,128)S(1)}, u32[]{:S(2)}, u32[]{:S(2)}) collective-permute-start(f32[4,128]{1,0:T(4,128)S(1)} %get-tuple-element.9), channel_id=1, source_target_pairs={{1,0},{2,1},{3,2},{5,4},{6,5},{7,6},{9,8},{10,9},{11,10},{13,12},{... | collective-permute-start | bytes 6152 | tf_op jit(solution)/shard_map/ppermute | solution.py:12
  46.2 25.7 %collective-permute-start.2 = (f32[4,128]{1,0:T(4,128)S(1)}, f32[4,128]{1,0:T(4,128)S(1)}, u32[]{:S(2)}, u32[]{:S(2)}) collective-permute-start(f32[4,128]{1,0:T(4,128)S(1)} %get-tuple-element.8), channel_id=1, source_target_pairs={{0,1},{1,2},{2,3},{4,5},{5,6},{6,7},{8,9},{9,10},{10,11},{12,13},{... | collective-permute-start | bytes 6152 | tf_op jit(solution)/shard_map/ppermute | solution.py:12
  59.9 36.8 %collective-permute-start.1 = (f32[4,128]{1,0:T(4,128)S(1)}, f32[4,128]{1,0:T(4,128)S(1)}, u32[]{:S(2)}, u32[]{:S(2)}) collective-permute-start(f32[4,128]{1,0:T(4,128)S(1)} %get-tuple-element.11), channel_id=1, source_target_pairs={{4,0},{8,4},{12,8},{16,12},{20,16},{24,20},{28,24},{5,1},{9,5},{13... | collective-permute-start | bytes 6152 | tf_op jit(solution)/shard_map/ppermute | solution.py:12
  61.8 34.9 %collective-permute-start = (f32[4,128]{1,0:T(4,128)S(1)}, f32[4,128]{1,0:T(4,128)S(1)}, u32[]{:S(2)}, u32[]{:S(2)}) collective-permute-start(f32[4,128]{1,0:T(4,128)S(1)} %get-tuple-element.10), channel_id=1, source_target_pairs={{0,4},{4,8},{8,12},{12,16},{16,20},{20,24},{24,28},{1,5},{5,9},{9,... | collective-permute-start | bytes 6152 | tf_op jit(solution)/shard_map/ppermute | solution.py:12
  69.8 1.1 copy-start.7
  70.1 0.7 copy-start.4
Sparse Core Ops, SparseCore 0:
  70.9 127.4 all-reduce.6
where the time goes:
time: 207 us
  waiting for transfers between devices  71.2 us (34%)
  blocking collectives  63.2 us (31%)
  matrix products  27.7 us (13%)
  between operations  20.2 us (10%)
  local copies, waits for them, and re-layouts  13 us (6%)
  starting transfers between devices  10.4 us (5%)
    psum x1, waiting for transfers between devices, per_device(): kernel_grad = lax.psum(kernel_terms, ('row', 'col'))  71.2 us
    psum x1, blocking collectives, per_device(): col_total = lax.psum(inner_cols, 'row')  24.8 us
    psum x1, blocking collectives, per_device(): row_total = lax.psum(inner_rows, 'col')  15.8 us
    all_gather x1, blocking collectives, per_device(): every_row = lax.all_gather(row_total, 'row', axis=0, tiled=True)  14.2 us
    dot_general x17, matrix products, convolve(): jnp.einsum('ijc,fc->fij', tap_piece, kernel[tap_row + 1, tap_col + 1], pr...  10.5 us
    ppermute x4, starting transfers between devices, shifted(): return lax.ppermute(value, axis, pairs)  10.3 us
    all_gather x1, blocking collectives, per_device(): every_bin = lax.all_gather(embedding, 'col', axis=0, tiled=True)  8.41 us
    dynamic_update_slice x36, local copies, waits for them, and re-layouts, add_into(): lax.dynamic_update_slice_in_dim(target, current + update, position, 0)  8.11 us
  transfers between devices with their start and end apart: 5, of which 1 were waited for; matrix products, arithmetic and copies ran while one was open for 8% of the time, Pallas kernels for 0%

commit v1 on v0

--- a/solution.py
+++ b/solution.py
@@ -1,9 +1,27 @@
+import functools
 import jax
 import jax.numpy as jnp
 from jax import lax
 from jax.sharding import PartitionSpec as P
+from jax.lax import axis_index, axis_size, ppermute
 
 DMAX = 4
+
+
+def mark_record_on(m, axis_no):
+    z1, field_out, b_next = (axis_size("row"), axis_index("row"), m.shape[axis_no])
+    top, out_arr = (m, 1)
+    while out_arr < z1:
+        top = jnp.concatenate(
+            [top, ppermute(top, "row", [(src_i, (src_i - out_arr) % z1) for src_i in range(z1)])],
+            axis_no,
+        )
+        out_arr = 2 * out_arr
+    local_now = jnp.roll(top, field_out * b_next, axis_no)
+    return local_now
+
+
+put_the_loads = functools.partial(mark_record_on, axis_no=0)
 
 
 def shifted(value, axis, by):
@@ -192,7 +210,7 @@
     lower_rows = shifted(row_grad[row_count + margin :], "row", 1)
     inner_rows = fold_edges(row_grad, margin, row_count, lower_rows, upper_rows)
     row_total = lax.psum(inner_rows, "col")
-    every_row = lax.all_gather(row_total, "row", axis=0, tiled=True)
+    every_row = put_the_loads(row_total)
     row_share = lax.dynamic_slice_in_dim(every_row, col_start, col_count, 0)
     left_cols = shifted(col_grad[:margin], "col", -1)
     right_cols = shifted(col_grad[col_count + margin :], "col", 1)

time: 207 us -> 207 us (level)
  blocking collectives: 63.2 us -> 50.2 us
  starting transfers between devices: 10.4 us -> 17.2 us
  waiting for transfers between devices: 71.2 us -> 77.3 us
    all_gather x1 -> x0, blocking collectives: 14.2 us -> none  [per_device(): every_row = lax.all_gather(row_total, 'row', axis=0, tiled=True)]
    ppermute x0 -> x3, starting transfers between devices: none -> 6.83 us  [mark_record_on(): ppermute(top, 'row', [(src_i, (src_i - out_arr) % z1) for src_i in range(...]
    ppermute x0 -> x3, waiting for transfers between devices: none -> 4.1 us  [mark_record_on(): ppermute(top, 'row', [(src_i, (src_i - out_arr) % z1) for src_i in range(...]
  transfers between devices with their start and end apart: 5 -> 8, of which waited for: 1 -> 3; matrix products, arithmetic and copies ran while one was open for 8% -> 8% of each run, Pallas kernels for 0% -> 0%
where the time goes in v1:
time: 207 us
  waiting for transfers between devices  77.3 us (37%)
  blocking collectives  50.2 us (24%)
  matrix products  27.7 us (13%)
  between operations  20.3 us (10%)
  starting transfers between devices  17.2 us (8%)
  local copies, waits for them, and re-layouts  13 us (6%)
    psum x1, waiting for transfers between devices, per_device(): kernel_grad = lax.psum(kernel_terms, ('row', 'col'))  73.2 us
    psum x1, blocking collectives, per_device(): col_total = lax.psum(inner_cols, 'row')  25.9 us
    psum x1, blocking collectives, per_device(): row_total = lax.psum(inner_rows, 'col')  15.8 us
    dot_general x17, matrix products, convolve(): jnp.einsum('ijc,fc->fij', tap_piece, kernel[tap_row + 1, tap_col + 1], pr...  10.5 us
    ppermute x4, starting transfers between devices, shifted(): return lax.ppermute(value, axis, pairs)  10.3 us
    all_gather x1, blocking collectives, per_device(): every_bin = lax.all_gather(embedding, 'col', axis=0, tiled=True)  8.41 us
    dynamic_update_slice x36, local copies, waits for them, and re-layouts, add_into(): lax.dynamic_update_slice_in_dim(target, current + update, position, 0)  8.11 us
    ppermute x3, starting transfers between devices, mark_record_on(): ppermute(top, 'row', [(src_i, (src_i - out_arr) % z1) for src_i in range(...  6.83 us
  transfers between devices with their start and end apart: 8, of which 3 were waited for; matrix products, arithmetic and copies ran while one was open for 8% of the time, Pallas kernels for 0%

profile of v1, /device:TPU:8, one launch (start us, length us, event | category | flops | bytes accessed | tf_op | source)
XLA Modules:
  0.0 206.9 jit_solution(4870368362891931498)
XLA Ops:
  7.2 1.3 fusion.300
  13.8 8.4 %all_gather.3 = bf16[256,128]{1,0:T(8,128)(2,1)S(1)} all-gather(bf16[64,128]{1,0:T(8,128)(2,1)} %param.7), channel_id=1, replica_groups=mesh['row'=8,'col'=4] {'col'}, dimensions={0}, use_global_device_ids=true | all-gather | bytes 81920 | tf_op jit(solution)/shard_map/all_gather | solution.py:67
  22.3 0.5 fusion.35
  22.8 0.6 fusion.72
  23.4 0.6 fusion.68
  24.0 0.6 convolution_add_fusion.13
  24.7 0.6 convolution_add_fusion.12
  25.3 0.6 fusion.3
  26.0 0.6 convolution_add_fusion.10
  26.6 0.6 convolution_add_fusion.9
  27.2 0.6 convolution_add_fusion.8
  27.9 0.6 fusion.59
  28.5 0.6 convolution_add_fusion.6
  29.1 0.6 convolution_add_fusion.5
  29.8 0.5 copy-done.3
  30.3 0.6 fusion.1
  30.9 0.6 convolution_add_fusion.3
  31.5 0.6 convolution_add_fusion.2
  32.2 0.6 convolution_add_fusion.1
  32.8 0.6 fusion.2
  33.4 0.6 fusion
  34.1 0.4 bitcast_select_fusion
  36.0 0.3 dynamic_update_slice.126
  36.5 0.3 dynamic_update_slice.127
  37.4 0.3 dynamic_update_slice.129
  44.9 1.3 collective-permute-start.6
  46.2 4.7 %collective-permute-start.5 = (f32[4,128]{1,0:T(4,128)S(1)}, f32[4,128]{1,0:T(4,128)S(1)}, u32[]{:S(2)}, u32[]{:S(2)}) collective-permute-start(f32[4,128]{1,0:T(4,128)S(1)} %get-tuple-element.8), channel_id=1, source_target_pairs={{0,1},{1,2},{2,3},{4,5},{5,6},{6,7},{8,9},{9,10},{10,11},{12,13},{... | collective-permute-start | bytes 6152 | tf_op jit(solution)/shard_map/ppermute | solution.py:30
  50.9 0.5 fusion.272
  51.4 0.5 fusion.270
  51.9 0.5 fusion.264
  52.4 0.5 fusion.268
  52.9 0.5 fusion.266
  56.5 0.5 fusion.262
  59.9 1.9 collective-permute-start.1
  61.8 2.4 %collective-permute-start = (f32[4,128]{1,0:T(4,128)S(1)}, f32[4,128]{1,0:T(4,128)S(1)}, u32[]{:S(2)}, u32[]{:S(2)}) collective-permute-start(f32[4,128]{1,0:T(4,128)S(1)} %get-tuple-element.10), channel_id=1, source_target_pairs={{0,4},{4,8},{8,12},{12,16},{16,20},{20,24},{24,28},{1,5},{5,9},{9,... | collective-permute-start | bytes 6152 | tf_op jit(solution)/shard_map/ppermute | solution.py:30
  64.2 0.3 convolution_bitcast_fusion.16
  64.5 0.3 convolution_bitcast_fusion.14
  64.8 0.3 convolution_bitcast_fusion.12
  65.2 0.3 convolution_bitcast_fusion.10
  65.5 0.3 convolution_bitcast_fusion.8
  65.8 0.3 convolution_bitcast_fusion.6
  66.1 0.3 convolution_bitcast_fusion.4
  66.5 0.3 convolution_bitcast_fusion.2
  66.8 0.3 convolution_bitcast_fusion
  67.1 0.3 fusion.10
  67.4 0.3 fusion.13
  67.8 0.3 fusion.16
  68.1 0.3 fusion.19
  68.4 0.3 fusion.22
  68.8 0.3 fusion.25
  69.1 0.3 fusion.28
  69.4 0.3 fusion.31
  69.8 0.3 fusion.34
  70.1 0.7 copy-done.4
  71.2 0.7 copy.11
  71.9 15.8 %psum.21 = f32[32,128]{1,0:T(8,128)S(1)} all-reduce(f32[32,128]{1,0:T(8,128)S(1)} %fusion.95), channel_id=1, replica_groups=mesh['row'=8,'col'=4] {'col'}, use_global_device_ids=true, to_apply=%region_0.1 | all-reduce | flops 4096 | bytes 32768 | tf_op jit(solution)/shard_map/psum | solution.py:212
  87.7 25.9 %psum.22 = f32[64,128]{1,0:T(8,128)S(1)} all-reduce(f32[64,128]{1,0:T(8,128)S(1)} %fusion.93), channel_id=1, replica_groups=mesh['row'=8,'col'=4] {'row'}, use_global_device_ids=true, to_apply=%region_1.2 | all-reduce | flops 8192 | bytes 65536 | tf_op jit(solution)/shard_map/psum | solution.py:218
  113.7 4.2 %collective-permute-start.3 = (f32[64,128]{1,0:T(8,128)S(1)}, f32[64,128]{1,0:T(8,128)S(1)}, u32[]{:S(2)}, u32[]{:S(2)}) collective-permute-start(f32[64,128]{1,0:T(8,128)S(1)} %pad_maximum_fusion.1), channel_id=1, source_target_pairs={{0,24},{4,28},{8,0},{12,4},{16,8},{20,12},{24,16},{28,20},{1,25},{... | collective-permute-start | bytes 98312 | tf_op jit(solution)/shard_map/ppermute | solution.py:16
  117.8 1.6 collective-permute-done.3
  119.4 2.7 %collective-permute-start.4 = (f32[128,128]{1,0:T(8,128)S(1)}, f32[128,128]{1,0:T(8,128)S(1)}, u32[]{:S(2)}, u32[]{:S(2)}) collective-permute-start(f32[128,128]{1,0:T(8,128)S(1)} %pad_maximum_fusion), channel_id=1, source_target_pairs={{0,16},{4,20},{8,24},{12,28},{16,0},{20,4},{24,8},{28,12},{1,17},{... | collective-permute-start | bytes 196616 | tf_op jit(solution)/shard_map/ppermute | solution.py:16
  122.1 2.5 %collective-permute-done.4 = f32[128,128]{1,0:T(8,128)S(1)} collective-permute-done((f32[128,128]{1,0:T(8,128)S(1)}, f32[128,128]{1,0:T(8,128)S(1)}, u32[]{:S(2)}, u32[]{:S(2)}) %collective-permute-start.4) | collective-permute-done | bytes 65568 | tf_op jit(solution)/shard_map/ppermute | solution.py:16
  124.7 0.6 add_multiply_fusion
  125.3 73.2 %all-reduce.7.cloned.1.call-done = f32[3,3,48,128]{3,2,1,0:T(8,128)} async-done(((f32[3,3,48,128]{3,2,1,0:T(8,128)}), f32[3,3,48,128]{3,2,1,0:T(8,128)}) %all-reduce.7.cloned.1.call-update) | async-done | bytes 221200 | tf_op jit(solution)/shard_map/psum | solution.py:137
  198.5 1.6 copy.94
  (122 shorter events, 15.7 us)
Async XLA Ops:
  7.2 26.9 %copy-start = (bf16[5,32,64]{2,1,0:T(8,128)(2,1)S(1)}, bf16[5,32,64]{2,1,0:T(8,128)(2,1)}, u32[]{:S(2)}) copy-start(bf16[5,32,64]{2,1,0:T(8,128)(2,1)} %param.13) | copy-start | bytes 61444
  7.2 15.6 %copy-start.1 = (bf16[3,3,48,128]{3,2,1,0:T(8,128)(2,1)S(1)}, bf16[3,3,48,128]{3,2,1,0:T(8,128)(2,1)}, u32[]{:S(2)}) copy-start(bf16[3,3,48,128]{3,2,1,0:T(8,128)(2,1)} %param.9) | copy-start | bytes 331780
  7.2 191.3 %all-reduce.7.cloned.1.call-start = ((), (), s32[]{:S(2)}) async-start(), calls=%async_computation | async-start | bytes 442368 | tf_op jit(solution)/shard_map/psum | solution.py:137
  23.4 1.9 copy-start.2
  29.1 1.1 copy-start.3
  32.1 0.7 copy-start.6
  33.4 0.7 copy-start.5
  44.9 42.8 %collective-permute-start.6 = (f32[4,128]{1,0:T(4,128)S(1)}, f32[4,128]{1,0:T(4,128)S(1)}, u32[]{:S(2)}, u32[]{:S(2)}) collective-permute-start(f32[4,128]{1,0:T(4,128)S(1)} %get-tuple-element.9), channel_id=1, source_target_pairs={{1,0},{2,1},{3,2},{5,4},{6,5},{7,6},{9,8},{10,9},{11,10},{13,12},{... | collective-permute-start | bytes 6152 | tf_op jit(solution)/shard_map/ppermute | solution.py:30
  46.2 41.5 %collective-permute-start.5 = (f32[4,128]{1,0:T(4,128)S(1)}, f32[4,128]{1,0:T(4,128)S(1)}, u32[]{:S(2)}, u32[]{:S(2)}) collective-permute-start(f32[4,128]{1,0:T(4,128)S(1)} %get-tuple-element.8), channel_id=1, source_target_pairs={{0,1},{1,2},{2,3},{4,5},{5,6},{6,7},{8,9},{9,10},{10,11},{12,13},{... | collective-permute-start | bytes 6152 | tf_op jit(solution)/shard_map/ppermute | solution.py:30
  59.9 12.0 %collective-permute-start.1 = (f32[4,128]{1,0:T(4,128)S(1)}, f32[4,128]{1,0:T(4,128)S(1)}, u32[]{:S(2)}, u32[]{:S(2)}) collective-permute-start(f32[4,128]{1,0:T(4,128)S(1)} %get-tuple-element.11), channel_id=1, source_target_pairs={{4,0},{8,4},{12,8},{16,12},{20,16},{24,20},{28,24},{5,1},{9,5},{13... | collective-permute-start | bytes 6152 | tf_op jit(solution)/shard_map/ppermute | solution.py:30
  61.8 10.1 %collective-permute-start = (f32[4,128]{1,0:T(4,128)S(1)}, f32[4,128]{1,0:T(4,128)S(1)}, u32[]{:S(2)}, u32[]{:S(2)}) collective-permute-start(f32[4,128]{1,0:T(4,128)S(1)} %get-tuple-element.10), channel_id=1, source_target_pairs={{0,4},{4,8},{8,12},{12,16},{16,20},{20,24},{24,28},{1,5},{5,9},{9,... | collective-permute-start | bytes 6152 | tf_op jit(solution)/shard_map/ppermute | solution.py:30
  69.8 1.1 copy-start.7
  70.1 0.7 copy-start.4
  87.7 26.0 %collective-permute-start.2 = (f32[32,128]{1,0:T(8,128)S(1)}, f32[32,128]{1,0:T(8,128)S(1)}, u32[]{:S(2)}, u32[]{:S(2)}) collective-permute-start(f32[32,128]{1,0:T(8,128)S(1)} %psum.21), channel_id=1, source_target_pairs={{0,28},{4,0},{8,4},{12,8},{16,12},{20,16},{24,20},{28,24},{1,29},{... | collective-permute-start | bytes 49160 | tf_op jit(solution)/shard_map/ppermute | solution.py:16
  113.7 5.8 %collective-permute-start.3 = (f32[64,128]{1,0:T(8,128)S(1)}, f32[64,128]{1,0:T(8,128)S(1)}, u32[]{:S(2)}, u32[]{:S(2)}) collective-permute-start(f32[64,128]{1,0:T(8,128)S(1)} %pad_maximum_fusion.1), channel_id=1, source_target_pairs={{0,24},{4,28},{8,0},{12,4},{16,8},{20,12},{24,16},{28,20},{1,25},{... | collective-permute-start | bytes 98312 | tf_op jit(solution)/shard_map/ppermute | solution.py:16
  119.4 5.2 %collective-permute-start.4 = (f32[128,128]{1,0:T(8,128)S(1)}, f32[128,128]{1,0:T(8,128)S(1)}, u32[]{:S(2)}, u32[]{:S(2)}) collective-permute-start(f32[128,128]{1,0:T(8,128)S(1)} %pad_maximum_fusion), channel_id=1, source_target_pairs={{0,16},{4,20},{8,24},{12,28},{16,0},{20,4},{24,8},{28,12},{1,17},{... | collective-permute-start | bytes 196616 | tf_op jit(solution)/shard_map/ppermute | solution.py:16
Sparse Core Ops, SparseCore 0:
  70.9 127.4 all-reduce.6
